TPU v7x, 256 devices: a whole 4x4x8 slice. The times are simulated.
256 devices in a mesh: group: 64 (over z, y, core), section: 4 (over x).
Axes of the slice: x: 4, y: 4, z: 8, core: 2. Of those that a mesh axis runs over, the one named last changes fastest.
Arguments:
- embed_in: bfloat16 [256, 32, 1792], P(('group', 'section')), may hold values from -6 to 6
- clean_cache: bfloat16 [4, 256, 32, 1792], P('section', 'group'), may hold values from -6 to 6
- lengths: int32 [256, 5], P(('group', 'section')), may hold values from 1 to 24, 32 in all within a row
- patch_layer: int32 [256, 4], P(('group', 'section')), may hold values from 0 to 3
- patch_pos: int32 [256, 4], P(('group', 'section')), may hold values from 0 to 31
- answers: int32 [256, 4, 2], P(('group', 'section')), may hold values from 0 to 77823
- attn_gain: float32 [4, 1792], P('section'), may hold values from 0.5 to 1.5
- w_query: bfloat16 [4, 1792, 1792], P('section', 'group'), may hold values from -0.125 to 0.125
- b_query: float32 [4, 1792], P('section'), may hold values from -3 to 3
- w_keyval: bfloat16 [4, 1792, 512], P('section', 'group'), may hold values from -0.125 to 0.125
- b_key: float32 [4, 256], P('section'), may hold values from -3 to 3
- b_value: float32 [4, 256], P('section'), may hold values from -3 to 3
- w_out: bfloat16 [4, 1792, 1792], P('section', 'group'), may hold values from -0.125 to 0.125
- final_gain: float32 [1792], replicated, may hold values from 0.5 to 1.5
- unembed: bfloat16 [77824, 1792], P(('group', 'section')), may hold values from -0.125 to 0.125
Outputs:
- final_resid: bfloat16 [256, 32, 1792], P(('group', 'section'))
- logit_diff: float32 [256, 4], P(('group', 'section'))
- cell_sums: float32 [4, 24], replicated
Inputs may be any that keep to these rules, and one draw needn't show every extreme that they name: Each row holds 4 prompt lengths followed by the padding of its bucket and sums to 32.
All inputs are finite; a program needn't handle non-finite values.
Results may differ from a plain program's by a relative error of at most 0.02.
Values may be sent and summed in bfloat16 or wider, within the bound.
No kernel may reach another device: no remote copies, remote signals or barrier semaphores. Data moves between devices by JAX's collectives and lax.ppermute only.
A program may use at most 128 MiB of HBM per device.

v0:
```python
import functools
import math
import jax
import jax.numpy as jnp
from jax import lax
from jax.sharding import Mesh
from jax.sharding import PartitionSpec as P

HQ = 14
KV = 2
HD = 128
MAXLEN = 24
GROUP = ("group_0", "group_1", "group_2")
GROUP_SECTION = ("group_0", "group_1", "group_2", "section")
epsilon = 1e-06
rope_base = 1000000.0


def from_behind(block, axis, distance):
    devices = range(lax.axis_size(axis))
    route = [(i - distance, i) for i in devices if i - distance in devices]
    return lax.ppermute(block, axis, route)


def in_one_piece(arrays, axis, dim, along):
    widths = [a.shape[along] for a in arrays]
    both = jnp.concatenate(arrays, axis=along)
    filled = lax.all_gather(both, axis, axis=dim, tiled=True)
    return tuple(jnp.split(filled, [sum(widths[:k]) for k in range(1, len(widths))], axis=along))


def sent_together(arrays, axis, dim, along):
    widths = [math.prod(a.shape[along:]) for a in arrays]
    both = jnp.concatenate(
        [a.reshape(*a.shape[:along], w) for a, w in zip(arrays, widths)], axis=along
    )
    filled = lax.all_gather(both, axis, axis=dim, tiled=True)
    blocks = jnp.split(filled, [sum(widths[:k]) for k in range(1, len(widths))], axis=along)
    return tuple(
        (b.reshape(*filled.shape[:along], *a.shape[along:]) for a, b in zip(arrays, blocks))
    )


def over_axes(value, axes):
    return functools.reduce(lax.psum, axes, value)


def rmsnorm(hidden, norm_gain):
    residual = hidden.astype(jnp.float32)
    scaled = residual * lax.rsqrt(jnp.mean(residual * residual, axis=-1, keepdims=True) + epsilon)
    return (scaled * norm_gain).astype(jnp.bfloat16)


def rotary(heads, position):
    half_dim = heads.shape[-1] // 2
    frequency = jnp.exp(jnp.arange(half_dim, dtype=jnp.float32) * (-math.log(rope_base) / half_dim))
    angles = position.astype(jnp.float32)[:, None] * frequency[None, :]
    cosine = jnp.cos(angles)[:, None, :]
    sinus = jnp.sin(angles)[:, None, :]
    front_half = heads[..., :half_dim]
    back_half = heads[..., half_dim:]
    return jnp.concatenate(
        [front_half * cosine - back_half * sinus, back_half * cosine + front_half * sinus], axis=-1
    )


def bucket_layout(lengths_rows, seq_len):
    end_rows = jnp.cumsum(lengths_rows, axis=-1).astype(jnp.int32)
    starts = (end_rows - lengths_rows).astype(jnp.int32)
    row_ids = jnp.arange(seq_len, dtype=jnp.int32)
    segment = jnp.sum((row_ids[:, None] >= end_rows[..., None, :]).astype(jnp.int32), axis=-1)
    slots = jnp.arange(lengths_rows.shape[-1], dtype=jnp.int32)
    member = segment[..., :, None] == slots
    position = row_ids - jnp.sum(jnp.where(member, starts[..., None, :], 0), axis=-1)
    return (segment, position, starts)


def patch_hits(starts, lengths_rows, layers, offsets, layer_now, seq_len):
    prompts = layers.shape[-1]
    target = (starts[..., :prompts] + offsets % lengths_rows[..., :prompts]).astype(jnp.int32)
    row_ids = jnp.arange(seq_len, dtype=jnp.int32)
    return jnp.any(
        (row_ids[:, None] == target[..., None, :]) & (layers[..., None, :] == layer_now), axis=-1
    )


def attend_piece(
    hidden,
    norm_gain,
    query_weight,
    query_bias,
    keyval_weight,
    key_bias,
    value_bias,
    output_weight,
    seg_query,
    pos_query,
    seg_keys,
    row_start,
    key_cache,
    value_cache,
):
    count_rows = hidden.shape[0]
    normed = rmsnorm(hidden, norm_gain)
    queries = jnp.dot(normed, query_weight, preferred_element_type=jnp.float32) + query_bias
    keyval = jnp.dot(normed, keyval_weight, preferred_element_type=jnp.float32)
    width_kv = keyval.shape[1] // 2
    keys_rot = rotary(
        (keyval[:, :width_kv] + key_bias).reshape(count_rows, KV, HD), pos_query
    ).astype(jnp.bfloat16)
    values_new = (
        (keyval[:, width_kv:] + value_bias).reshape(count_rows, KV, HD).astype(jnp.bfloat16)
    )
    queries_rot = rotary(queries.reshape(count_rows, HQ, HD), pos_query).astype(jnp.bfloat16)
    queries_rot = queries_rot.reshape(count_rows, KV, HQ // KV, HD)
    key_cache = keys_rot
    value_cache = values_new
    scores = jnp.einsum(
        "qgrd,kgd->grqk", queries_rot, key_cache, preferred_element_type=jnp.float32
    ) * HD ** (-0.5)
    query_ids = row_start + jnp.arange(count_rows, dtype=jnp.int32)
    key_ids = jnp.arange(key_cache.shape[0], dtype=jnp.int32)
    allowed = (seg_query[:, None] == seg_keys[None, :]) & (key_ids[None, :] <= query_ids[:, None])
    scores = jnp.where(allowed, scores, -1e30)
    weights = jax.nn.softmax(scores, axis=-1).astype(jnp.bfloat16)
    attended = jnp.einsum(
        "grqk,kgd->qgrd", weights, value_cache, preferred_element_type=jnp.float32
    )
    attended = attended.astype(jnp.bfloat16).reshape(count_rows, HQ * HD)
    updated = hidden.astype(jnp.float32) + jnp.dot(
        attended, output_weight, preferred_element_type=jnp.float32
    )
    return (updated.astype(jnp.bfloat16), key_cache, value_cache)


def pass_on(hidden):
    return from_behind(hidden, "section", 1)


def answer_terms(readout_all, answer_ids, unembed, offset):
    logits = lax.dot_general(
        readout_all, unembed, (((1,), (1,)), ((), ())), preferred_element_type=jnp.float32
    )
    vocab_ids = offset + jnp.arange(unembed.shape[0], dtype=jnp.int32)
    choosing = (answer_ids[:, 0:1] == vocab_ids[None, :]).astype(jnp.float32) - (
        answer_ids[:, 1:2] == vocab_ids[None, :]
    ).astype(jnp.float32)
    return jnp.sum(logits * choosing, axis=1)


def cell_table(answer_diffs, cell_ids, cell_count):
    onehot = (cell_ids[:, None] == jnp.arange(cell_count, dtype=jnp.int32)[None, :]).astype(
        jnp.float32
    )
    return jnp.dot(answer_diffs, onehot, precision=lax.Precision.HIGHEST)


def per_device(
    embed_in,
    clean_cache,
    lengths,
    patch_layer,
    patch_pos,
    answers,
    attn_gain,
    w_query,
    b_query,
    w_keyval,
    b_key,
    b_value,
    w_out,
    final_gain,
    unembed,
):
    section_count = lax.axis_size("section")
    section_index = lax.axis_index("section")
    seq_len = embed_in.shape[1]
    feature_count = embed_in.shape[2]
    prompts = patch_layer.shape[1]
    inputs, lens_all, layer_all, offset_all = (
        lax.all_gather(embed_in, "section", axis=0, tiled=True),
        *in_one_piece((lengths, patch_layer, patch_pos), "section", 0, 1),
    )
    query_weight, keyval_weight, output_weight = in_one_piece(
        (w_query[0], w_keyval[0], w_out[0]), GROUP, 0, 1
    )
    segment, position, starts = bucket_layout(lens_all, seq_len)
    hits = patch_hits(starts, lens_all, layer_all, offset_all, section_index, seq_len)
    pieces = 1
    piece_rows = seq_len // pieces
    piece_total = section_count * pieces
    tick_count = section_count + piece_total - 1
    key_cache = jnp.zeros((seq_len, KV, HD), jnp.bfloat16)
    value_cache = jnp.zeros((seq_len, KV, HD), jnp.bfloat16)
    finished = jnp.zeros((section_count, seq_len, feature_count), jnp.bfloat16)
    moving = jnp.zeros((piece_rows, feature_count), jnp.bfloat16)
    for moment in range(tick_count):
        piece_order = moment - section_index
        in_range = (piece_order >= 0) & (piece_order < piece_total)
        clamped = jnp.clip(piece_order, 0, piece_total - 1)
        bucket = clamped // pieces
        row_start = clamped % pieces * piece_rows
        fresh_rows = lax.dynamic_slice(
            inputs, (bucket, row_start, 0), (1, piece_rows, feature_count)
        )[0]
        current = jnp.where(section_index == 0, fresh_rows, moving)
        clean_rows = lax.dynamic_slice(
            clean_cache[0], (bucket, row_start, 0), (1, piece_rows, feature_count)
        )[0]
        patched = lax.dynamic_slice(hits, (bucket, row_start), (1, piece_rows))[0]
        current = jnp.where(patched[:, None], clean_rows, current)
        seg_keys = lax.dynamic_slice_in_dim(segment, bucket, 1, 0)[0]
        pos_bucket = lax.dynamic_slice_in_dim(position, bucket, 1, 0)[0]
        result, key_cache, value_cache = attend_piece(
            current,
            attn_gain[0],
            query_weight,
            b_query[0],
            keyval_weight,
            b_key[0],
            b_value[0],
            output_weight,
            seg_keys,
            pos_bucket,
            seg_keys,
            row_start,
            key_cache,
            value_cache,
        )
        stored = lax.dynamic_update_slice(finished, result[None], (bucket, row_start, 0))
        finished = jnp.where(in_range & (section_index == section_count - 1), stored, finished)
        if moment + 1 < tick_count:
            moving = pass_on(result)
    received = lax.all_to_all(finished, "section", split_axis=0, concat_axis=0, tiled=True)
    own_rows = received[section_count - 1 : section_count]
    own_lengths = lengths[0]
    own_starts = jnp.cumsum(own_lengths) - own_lengths
    last_rows = own_starts[:prompts] + own_lengths[:prompts] - 1
    readout = rmsnorm(own_rows[0][last_rows], final_gain)
    distance = own_lengths[:prompts] - 1 - patch_pos[0] % own_lengths[:prompts]
    cell_ids = patch_layer[0] * MAXLEN + distance
    cell_count = section_count * MAXLEN
    offset = lax.axis_index(GROUP_SECTION) * unembed.shape[0]
    readout_all, answer_ids, cells_all = (
        lax.all_gather(readout, GROUP_SECTION, axis=0, tiled=True),
        *sent_together((answers[0], cell_ids), GROUP_SECTION, 0, 1),
    )
    partial_value = answer_terms(readout_all, answer_ids, unembed, offset)
    answer_diffs = over_axes(partial_value, GROUP_SECTION)
    own_diff = lax.dynamic_slice_in_dim(
        answer_diffs, lax.axis_index(GROUP_SECTION) * prompts, prompts, 0
    )
    cell_totals = cell_table(answer_diffs, cells_all, cell_count)
    return (own_rows, own_diff.reshape(1, prompts), cell_totals.reshape(section_count, MAXLEN))


def solution(mesh):
    torus = Mesh(
        mesh.devices.reshape(8, 4, 2, mesh.shape["section"]),
        ("group_0", "group_1", "group_2", "section"),
    )
    in_specs = (
        P(GROUP_SECTION, None, None),
        P("section", GROUP, None, None),
        P(GROUP_SECTION, None),
        P(GROUP_SECTION, None),
        P(GROUP_SECTION, None),
        P(GROUP_SECTION, None, None),
        P("section", None),
        P("section", GROUP, None),
        P("section", None),
        P("section", GROUP, None),
        P("section", None),
        P("section", None),
        P("section", GROUP, None),
        P(),
        P(GROUP_SECTION, None),
    )
    out_specs = (P(GROUP_SECTION, None, None), P(GROUP_SECTION, None), P())
    return jax.shard_map(
        per_device, mesh=torus, in_specs=in_specs, out_specs=out_specs, check_vma=False
    )
```

profile of v0, /device:TPU:2, one launch (start us, length us, event | category | flops | bytes accessed | tf_op | source)
XLA Modules:
  0.0 440.4 jit_solution(10479632377378621470)
XLA Ops:
  9.8 9.2 %all-gather = s32[4,1,13]{2,1,0:T(1,128)S(1)} all-gather(s32[1,1,13]{2,1,0:T(1,128)S(1)} %add_bitcast_fusion), channel_id=1, replica_groups=mesh['group_0'=8,'group_1'=4,'group_2'=2,'section'=4] {'section'}, dimensions={0}, use_global_device_ids=true | all-gather | bytes 260 | tf_op jit(solution)/shard_map/all_gather | solution.py:28
  21.5 12.2 %all_gather.16 = bf16[4,32,1792]{2,1,0:T(8,128)(2,1)S(1)} all-gather(bf16[1,32,1792]{2,1,0:T(8,128)(2,1)} %param.15), channel_id=1, replica_groups=mesh['group_0'=8,'group_1'=4,'group_2'=2,'section'=4] {'section'}, dimensions={0}, use_global_device_ids=true | all-gather | bytes 573440 | tf_op jit(solution)/shard_map/all_gather | solution.py:181
  35.4 77.6 %all-gather.7.cloned.1.call-done = bf16[64,28,4096]{2,1,0:T(8,128)(2,1)} async-done(((bf16[1,28,4096]{2,1,0:T(8,128)(2,1)}), bf16[64,28,4096]{2,1,0:T(8,128)(2,1)}) %all-gather.7.cloned.1.call-update) | async-done | bytes 14680080 | tf_op jit(solution)/shard_map/all_gather | solution.py:28
  113.0 17.5 %reshape.771 = bf16[1792,4096]{1,0:T(8,128)(2,1)} reshape(bf16[64,28,4096]{2,1,0:T(8,128)(2,1)} %all-gather.7.cloned.1.call-done) | data formatting | bytes 29360128
  139.0 4.7 %bitcast_dynamic-update-slice_fusion = (bf16[4,32,1792]{2,1,0:T(8,128)(2,1)}, bf16[32,1792]{1,0:T(8,128)(2,1)S(1)}) fusion(bf16[4,32,1792]{2,1,0:T(8,128)(2,1)} %broadcast_in_dim.116, s32[]{:T(128)S(6)} %min.22, pred[]{:T(512)S(6)} %and.121, bf16[32,1792]{1,0:T(8,128)(2,1)S(1)} %reshape.736, bf16[1792,4096]{1,0:T(8,128)(2,1)} %reshape.771, ...), kind=kOutput, calls=%fused_computation.214 | convolution fusion | flops 205750272 | bytes 6881285 | tf_op jit(solution)/shard_map/dot_general | solution.py:130
  153.1 4.1 convolution_add_fusion.11
  158.9 4.7 %fusion.133 = (bf16[4,32,1792]{2,1,0:T(8,128)(2,1)}, bf16[32,1792]{1,0:T(8,128)(2,1)S(1)}) fusion(bf16[4,32,1792]{2,1,0:T(8,128)(2,1)} %get-tuple-element.123, s32[]{:T(128)S(6)} %min.23, pred[]{:T(512)S(6)} %and.127, bf16[32,1792]{1,0:T(8,128)(2,1)S(1)} %reshape.739, bf16[1792,4096]{1,0:T(8,128)(2,1)} %reshape.771, bf16[32,1792]{1,0:T(8,128)(2,1)S(1)} %get-tuple-element.14), kind=kOutput, calls=%fused_computation.211 | convolution fusion | flops 205750272 | bytes 6995973 | tf_op jit(solution)/shard_map/dot_general | solution.py:130
  172.4 4.1 convolution_add_fusion.9
  178.2 4.7 %fusion.131 = (bf16[4,32,1792]{2,1,0:T(8,128)(2,1)}, bf16[32,1792]{1,0:T(8,128)(2,1)S(1)}) fusion(bf16[4,32,1792]{2,1,0:T(8,128)(2,1)} %get-tuple-element.125, s32[]{:T(128)S(6)} %min.24, pred[]{:T(512)S(6)} %and.130, bf16[32,1792]{1,0:T(8,128)(2,1)S(1)} %reshape.742, bf16[1792,4096]{1,0:T(8,128)(2,1)} %reshape.771, bf16[32,1792]{1,0:T(8,128)(2,1)S(1)} %get-tuple-element.12), kind=kOutput, calls=%fused_computation.207 | convolution fusion | flops 205750272 | bytes 6995973 | tf_op jit(solution)/shard_map/dot_general | solution.py:130
  197.6 4.7 %fusion.129 = (bf16[4,32,1792]{2,1,0:T(8,128)(2,1)}, bf16[32,1792]{1,0:T(8,128)(2,1)S(1)}) fusion(bf16[4,32,1792]{2,1,0:T(8,128)(2,1)} %get-tuple-element.127, s32[]{:T(128)S(6)} %min.25, pred[]{:T(512)S(6)} %and.133, bf16[32,1792]{1,0:T(8,128)(2,1)S(1)} %reshape.745, bf16[1792,4096]{1,0:T(8,128)(2,1)} %reshape.771, bf16[32,1792]{1,0:T(8,128)(2,1)S(1)} %get-tuple-element.10), kind=kOutput, calls=%fused_computation.203 | convolution fusion | flops 205750272 | bytes 6995973 | tf_op jit(solution)/shard_map/dot_general | solution.py:130
  211.1 4.1 convolution_add_fusion.5
  216.9 4.7 %fusion.127 = (bf16[4,32,1792]{2,1,0:T(8,128)(2,1)}, bf16[32,1792]{1,0:T(8,128)(2,1)S(1)}) fusion(bf16[4,32,1792]{2,1,0:T(8,128)(2,1)} %get-tuple-element.129, s32[]{:T(128)S(6)} %min.26, pred[]{:T(512)S(6)} %and.136, bf16[32,1792]{1,0:T(8,128)(2,1)S(1)} %reshape.748, bf16[1792,4096]{1,0:T(8,128)(2,1)} %reshape.771, bf16[32,1792]{1,0:T(8,128)(2,1)S(1)} %get-tuple-element.8), kind=kOutput, calls=%fused_computation.199 | convolution fusion | flops 205750272 | bytes 6995973 | tf_op jit(solution)/shard_map/dot_general | solution.py:130
  230.5 4.1 convolution_add_fusion.3
  236.3 4.7 %fusion.125 = (bf16[4,32,1792]{2,1,0:T(8,128)(2,1)}, bf16[32,1792]{1,0:T(8,128)(2,1)S(1)}) fusion(bf16[4,32,1792]{2,1,0:T(8,128)(2,1)} %get-tuple-element.131, s32[]{:T(128)S(6)} %min.27, pred[]{:T(512)S(6)} %and.139, bf16[32,1792]{1,0:T(8,128)(2,1)S(1)} %reshape.751, bf16[1792,4096]{1,0:T(8,128)(2,1)} %reshape.771, bf16[32,1792]{1,0:T(8,128)(2,1)S(1)} %get-tuple-element.6), kind=kOutput, calls=%fused_computation.195 | convolution fusion | flops 205750272 | bytes 6995973 | tf_op jit(solution)/shard_map/dot_general | solution.py:130
  249.8 4.1 convolution_add_fusion.1
  255.6 4.7 %fusion.16 = bf16[4,32,1792]{2,1,0:T(8,128)(2,1)} fusion(bf16[4,32,1792]{2,1,0:T(8,128)(2,1)} %get-tuple-element.133, s32[]{:T(128)S(6)} %min.28, bf16[32,1792]{1,0:T(8,128)(2,1)S(1)} %reshape.754, bf16[1792,4096]{1,0:T(8,128)(2,1)} %reshape.771, bf16[32,1792]{1,0:T(8,128)(2,1)S(1)} %get-tuple-element.4, pred[]{:T(512)S(6)} %and.142), kind=kOutput, calls=%fused_computation.31 | convolution fusion | flops 205750272 | bytes 6881285 | tf_op jit(solution)/shard_map/dot_general | solution.py:130
  260.4 4.8 %all-to-all-start = ((bf16[4,32,1792]{2,1,0:T(8,128)(2,1)}), bf16[4,32,1792]{2,1,0:T(8,128)(2,1)S(1)}, u32[]{:S(2)}, u32[]{:S(2)}) async-start(bf16[4,32,1792]{2,1,0:T(8,128)(2,1)} %fusion.16), calls=%async_computation | async-start | bytes 917504 | tf_op jit(solution)/shard_map/all_to_all | solution.py:234
  265.2 6.2 %all-to-all-done = bf16[4,32,1792]{2,1,0:T(8,128)(2,1)S(1)} async-done(((bf16[4,32,1792]{2,1,0:T(8,128)(2,1)}), bf16[4,32,1792]{2,1,0:T(8,128)(2,1)S(1)}, u32[]{:S(2)}, u32[]{:S(2)}) %all-to-all-start) | async-done | bytes 458784 | tf_op jit(solution)/shard_map/all_to_all | solution.py:234
  273.1 69.3 %all-gather.3 = s32[256,4,3]{2,1,0:T(4,128)S(1)} all-gather(s32[1,4,3]{2,1,0:T(4,128)S(1)} %bitcast.456), channel_id=1, replica_groups=mesh['group_0'=8,'group_1'=4,'group_2'=2,'section'=4] {'group_0','group_..., dimensions={0}, use_global_device_ids=true | all-gather | bytes 12336 | tf_op jit(solution)/shard_map/all_gather | solution.py:37
  344.0 40.0 %all-gather.9.cloned.1.call-done = bf16[256,4,1792]{2,1,0:T(4,128)(2,1)} async-done(((bf16[1,4,1792]{2,1,0:T(4,128)(2,1)}), bf16[256,4,1792]{2,1,0:T(4,128)(2,1)}) %all-gather.9.cloned.1.call-update) | async-done | bytes 3670032 | tf_op jit(solution)/shard_map/all_gather | solution.py:245
  384.1 6.9 %reshape.773 = bf16[1024,1792]{1,0:T(8,128)(2,1)} reshape(bf16[256,4,1792]{2,1,0:T(4,128)(2,1)} %all-gather.9.cloned.1.call-done) | data formatting | bytes 7340032
  394.3 16.0 %psum.28 = f32[1024]{0:T(1024)S(1)} all-reduce(f32[1024]{0:T(1024)S(1)} %fusion.31), channel_id=1, replica_groups=mesh['group_0'=8,'group_1'=4,'group_2'=2,'section'=4] {'group_0'}, use_global_device_ids=true, to_apply=%region_28.29 | all-reduce | flops 1024 | bytes 8192 | tf_op jit(solution)/shard_map/psum | solution.py:45
  410.4 9.7 %psum.29 = f32[1024]{0:T(1024)S(1)} all-reduce(f32[1024]{0:T(1024)S(1)} %psum.28), channel_id=1, replica_groups=mesh['group_0'=8,'group_1'=4,'group_2'=2,'section'=4] {'group_1'}, use_global_device_ids=true, to_apply=%region_29.30 | all-reduce | flops 1024 | bytes 8192 | tf_op jit(solution)/shard_map/psum | solution.py:45
  422.5 9.4 %psum.31 = f32[1024]{0:T(1024)S(1)} all-reduce(f32[1024]{0:T(1024)S(1)} %psum.30), channel_id=1, replica_groups=mesh['group_0'=8,'group_1'=4,'group_2'=2,'section'=4] {'section'}, use_global_device_ids=true, to_apply=%region_31.32 | all-reduce | flops 1024 | bytes 8192 | tf_op jit(solution)/shard_map/psum | solution.py:45
  (195 shorter events, 93.1 us)
Async XLA Ops:
  7.2 383.8 %copy-start = (bf16[304,1792]{1,0:T(8,128)(2,1)S(1)}, bf16[304,1792]{1,0:T(8,128)(2,1)}, u32[]{:S(2)}) copy-start(bf16[304,1792]{1,0:T(8,128)(2,1)} %param.29) | copy-start | bytes 3268612
  7.2 105.8 %all-gather.7.cloned.1.call-start = ((), (), s32[]{:S(2)}) async-start(), calls=%async_computation.1 | async-start | bytes 17039360 | tf_op jit(solution)/shard_map/all_gather | solution.py:28
  35.4 97.0 %copy-start.2 = (f32[1,256]{1,0:T(1,128)S(1)}, f32[1,256]{1,0:T(1,128)}, u32[]{:S(2)}) copy-start(f32[1,256]{1,0:T(1,128)} %param.26) | copy-start | bytes 3076
  35.4 97.0 %copy-start.3 = (f32[1,256]{1,0:T(1,128)S(1)}, f32[1,256]{1,0:T(1,128)}, u32[]{:S(2)}) copy-start(f32[1,256]{1,0:T(1,128)} %param.25) | copy-start | bytes 3076
  136.7 14.2 %copy-start.1 = (bf16[1,4,32,1792]{3,2,1,0:T(8,128)(2,1)S(1)}, bf16[1,4,32,1792]{3,2,1,0:T(8,128)(2,1)}, u32[]{:S(2)}) copy-start(bf16[1,4,32,1792]{3,2,1,0:T(8,128)(2,1)} %param.16) | copy-start | bytes 1376260
  143.7 7.2 %collective-permute-start = (bf16[32,1792]{1,0:T(8,128)(2,1)S(1)}, bf16[32,1792]{1,0:T(8,128)(2,1)S(1)}, u32[]{:S(2)}, u32[]{:S(2)}) collective-permute-start(bf16[32,1792]{1,0:T(8,128)(2,1)S(1)} %get-tuple-element.124), channel_id=1, source_target_pairs={{0,1},{1,2},{2,3},{4,5},{5,6},{6,7},{8,9},{9,10},{10,11},{12,13},{... | collective-permute-start | bytes 344072 | tf_op jit(solution)/shard_map/ppermute | solution.py:22
  163.6 6.7 %collective-permute-start.1 = (bf16[32,1792]{1,0:T(8,128)(2,1)S(1)}, bf16[32,1792]{1,0:T(8,128)(2,1)S(1)}, u32[]{:S(2)}, u32[]{:S(2)}) collective-permute-start(bf16[32,1792]{1,0:T(8,128)(2,1)S(1)} %get-tuple-element.126), channel_id=1, source_target_pairs={{0,1},{1,2},{2,3},{4,5},{5,6},{6,7},{8,9},{9,10},{10,11},{12,13},{... | collective-permute-start | bytes 344072 | tf_op jit(solution)/shard_map/ppermute | solution.py:22
  182.9 6.7 %collective-permute-start.2 = (bf16[32,1792]{1,0:T(8,128)(2,1)S(1)}, bf16[32,1792]{1,0:T(8,128)(2,1)S(1)}, u32[]{:S(2)}, u32[]{:S(2)}) collective-permute-start(bf16[32,1792]{1,0:T(8,128)(2,1)S(1)} %get-tuple-element.128), channel_id=1, source_target_pairs={{0,1},{1,2},{2,3},{4,5},{5,6},{6,7},{8,9},{9,10},{10,11},{12,13},{... | collective-permute-start | bytes 344072 | tf_op jit(solution)/shard_map/ppermute | solution.py:22
  202.3 6.7 %collective-permute-start.3 = (bf16[32,1792]{1,0:T(8,128)(2,1)S(1)}, bf16[32,1792]{1,0:T(8,128)(2,1)S(1)}, u32[]{:S(2)}, u32[]{:S(2)}) collective-permute-start(bf16[32,1792]{1,0:T(8,128)(2,1)S(1)} %get-tuple-element.130), channel_id=1, source_target_pairs={{0,1},{1,2},{2,3},{4,5},{5,6},{6,7},{8,9},{9,10},{10,11},{12,13},{... | collective-permute-start | bytes 344072 | tf_op jit(solution)/shard_map/ppermute | solution.py:22
  221.6 6.7 %collective-permute-start.4 = (bf16[32,1792]{1,0:T(8,128)(2,1)S(1)}, bf16[32,1792]{1,0:T(8,128)(2,1)S(1)}, u32[]{:S(2)}, u32[]{:S(2)}) collective-permute-start(bf16[32,1792]{1,0:T(8,128)(2,1)S(1)} %get-tuple-element.132), channel_id=1, source_target_pairs={{0,1},{1,2},{2,3},{4,5},{5,6},{6,7},{8,9},{9,10},{10,11},{12,13},{... | collective-permute-start | bytes 344072 | tf_op jit(solution)/shard_map/ppermute | solution.py:22
  234.6 10.0 %copy-start.7 = (s32[1,5]{1,0:T(1,128)S(1)}, s32[1,5]{1,0:T(1,128)}, u32[]{:S(2)}) copy-start(s32[1,5]{1,0:T(1,128)} %param.17) | copy-start | bytes 64
  241.0 6.7 %collective-permute-start.5 = (bf16[32,1792]{1,0:T(8,128)(2,1)S(1)}, bf16[32,1792]{1,0:T(8,128)(2,1)S(1)}, u32[]{:S(2)}, u32[]{:S(2)}) collective-permute-start(bf16[32,1792]{1,0:T(8,128)(2,1)S(1)} %get-tuple-element.134), channel_id=1, source_target_pairs={{0,1},{1,2},{2,3},{4,5},{5,6},{6,7},{8,9},{9,10},{10,11},{12,13},{... | collective-permute-start | bytes 344072 | tf_op jit(solution)/shard_map/ppermute | solution.py:22
  254.1 18.1 %copy-start.4 = (f32[1792]{0:T(1024)S(1)}, f32[1792]{0:T(1024)}, u32[]{:S(2)}) copy-start(f32[1792]{0:T(1024)} %param.28) | copy-start | bytes 21508
  254.1 18.8 %copy-start.5 = (s32[1,4]{1,0:T(1,128)S(1)}, s32[1,4]{1,0:T(1,128)}, u32[]{:S(2)}) copy-start(s32[1,4]{1,0:T(1,128)} %param.19) | copy-start | bytes 52
  254.1 18.8 %copy-start.6 = (s32[1,4]{1,0:T(1,128)S(1)}, s32[1,4]{1,0:T(1,128)}, u32[]{:S(2)}) copy-start(s32[1,4]{1,0:T(1,128)} %param.18) | copy-start | bytes 52
  254.1 18.9 %copy-start.8 = (s32[1,4,2]{1,2,0:T(2,128)S(1)}, s32[1,4,2]{1,2,0:T(2,128)}, u32[]{:S(2)}) copy-start(s32[1,4,2]{1,2,0:T(2,128)} %param.20) | copy-start | bytes 100
  260.4 11.1 %all-to-all-start = ((bf16[4,32,1792]{2,1,0:T(8,128)(2,1)}), bf16[4,32,1792]{2,1,0:T(8,128)(2,1)S(1)}, u32[]{:S(2)}, u32[]{:S(2)}) async-start(bf16[4,32,1792]{2,1,0:T(8,128)(2,1)} %fusion.16), calls=%async_computation | async-start | bytes 917504 | tf_op jit(solution)/shard_map/all_to_all | solution.py:234
  265.2 118.9 %all-gather.9.cloned.1.call-start = ((), (), s32[]{:S(2)}) async-start(), calls=%async_computation.2 | async-start | bytes 3684352 | tf_op jit(solution)/shard_map/all_gather | solution.py:245
Sparse Core Ops, SparseCore 0:
  10.8 102.1 all-gather.6
  273.0 111.0 all-gather.8
where the time goes:
time: 442 us; the launch traced here: 440 us
  waiting for transfers between devices  143 us (32%)
  blocking collectives  128 us (29%)
  matrix products  85.8 us (19%)
  local copies, waits for them, and re-layouts  32 us (7%)
  starting transfers between devices  25.4 us (6%)
  between operations  14.9 us (3%)
  other arithmetic  10.6 us (2%)
    all_gather x1, waiting for transfers between devices, in_one_piece(): filled = lax.all_gather(both, axis, axis=dim, tiled=True)  77.6 us
    all_gather x1, blocking collectives, sent_together(): filled = lax.all_gather(both, axis, axis=dim, tiled=True)  69.3 us
    all_gather x1, waiting for transfers between devices, per_device(): lax.all_gather(readout, GROUP_SECTION, axis=0, tiled=True)  40 us
    psum x4, blocking collectives, over_axes(): return functools.reduce(lax.psum, axes, value)  37.6 us
    dot_general x7, matrix products, attend_piece(): jnp.dot(attended, output_weight, preferred_element_type=jnp.float32)  33 us
    dot_general x7, matrix products, attend_piece(): jnp.dot(normed, query_weight, preferred_element_type=jnp.float32)  28.7 us
    unnamed x23, local copies, waits for them, and re-layouts  25 us
    ppermute x6, starting transfers between devices, from_behind(): return lax.ppermute(block, axis, route)  20.5 us
  transfers between devices with their start and end apart: 9, of which 9 were waited for; matrix products, arithmetic and copies ran while one was open for 2% of the time, Pallas kernels for 0%

commit v1 on v0

--- a/solution.py
+++ b/solution.py
@@ -242,7 +242,12 @@
     cell_count = section_count * MAXLEN
     offset = lax.axis_index(GROUP_SECTION) * unembed.shape[0]
     readout_all, answer_ids, cells_all = (
-        lax.all_gather(readout, GROUP_SECTION, axis=0, tiled=True),
+        jnp.concatenate(
+            lax.all_to_all(
+                jnp.stack([readout] * lax.axis_size(GROUP_SECTION)), GROUP_SECTION, 0, 0
+            ),
+            axis=0,
+        ),
         *sent_together((answers[0], cell_ids), GROUP_SECTION, 0, 1),
     )
     partial_value = answer_terms(readout_all, answer_ids, unembed, offset)

time: 442 us -> 485 us (1.097)
  blocking collectives: 128 us -> 199 us
  waiting for transfers between devices: 143 us -> 103 us
  starting transfers between devices: 25.4 us -> 34.2 us
    all_gather x1, blocking collectives: 69.3 us -> 143 us  [sent_together(): filled = lax.all_gather(both, axis, axis=dim, tiled=True)]
    all_gather x1 -> x0, waiting for transfers between devices: 40 us -> none  [per_device(): lax.all_gather(readout, GROUP_SECTION, axis=0, tiled=True)]
    all_to_all x0 -> x1, starting transfers between devices: none -> 8.7 us  [per_device(): lax.all_to_all(jnp.stack([readout] * lax.axis_size(GROUP_SECTION)), GROUP...]
    unnamed x23 -> x22, local copies, waits for them, and re-layouts: 25 us -> 18.1 us
    reshape x0 -> x1, local copies, waits for them, and re-layouts: none -> 6.87 us  [per_device(): jnp.concatenate(lax.all_to_all(jnp.stack([readout] * lax.axis_size(GROUP_...]
  transfers between devices with their start and end apart: 9 -> 9, of which waited for: 9 -> 8; matrix products, arithmetic and copies ran while one was open for 2% -> 1% of each run, Pallas kernels for 0% -> 0%
where the time goes in v1:
time: 485 us; the launch traced here: 482 us
  blocking collectives  199 us (41%)
  waiting for transfers between devices  103 us (21%)
  matrix products  85.8 us (18%)
  local copies, waits for them, and re-layouts  34.8 us (7%)
  starting transfers between devices  34.2 us (7%)
  between operations  14.9 us (3%)
  other arithmetic  10 us (2%)
    all_gather x1, blocking collectives, sent_together(): filled = lax.all_gather(both, axis, axis=dim, tiled=True)  143 us
    all_gather x1, waiting for transfers between devices, in_one_piece(): filled = lax.all_gather(both, axis, axis=dim, tiled=True)  77.6 us
    psum x4, blocking collectives, over_axes(): return functools.reduce(lax.psum, axes, value)  35.3 us
    dot_general x7, matrix products, attend_piece(): jnp.dot(attended, output_weight, preferred_element_type=jnp.float32)  33 us
    dot_general x7, matrix products, attend_piece(): jnp.dot(normed, query_weight, preferred_element_type=jnp.float32)  28.7 us
    ppermute x6, starting transfers between devices, from_behind(): return lax.ppermute(block, axis, route)  20.5 us
    ppermute x6, waiting for transfers between devices, from_behind(): return lax.ppermute(block, axis, route)  19.5 us
    unnamed x22, local copies, waits for them, and re-layouts  18.1 us
  transfers between devices with their start and end apart: 9, of which 8 were waited for; matrix products, arithmetic and copies ran while one was open for 1% of the time, Pallas kernels for 0%

profile of v1, /device:TPU:2, one launch (start us, length us, event | category | flops | bytes accessed | tf_op | source)
XLA Modules:
  0.0 482.3 jit_solution(13625747258177362325)
XLA Ops:
  9.8 9.2 %all-gather = s32[4,1,13]{2,1,0:T(1,128)S(1)} all-gather(s32[1,1,13]{2,1,0:T(1,128)S(1)} %add_bitcast_fusion), channel_id=1, replica_groups=mesh['group_0'=8,'group_1'=4,'group_2'=2,'section'=4] {'section'}, dimensions={0}, use_global_device_ids=true | all-gather | bytes 260 | tf_op jit(solution)/shard_map/all_gather | solution.py:28
  21.5 12.2 %all_gather.13 = bf16[4,32,1792]{2,1,0:T(8,128)(2,1)S(1)} all-gather(bf16[1,32,1792]{2,1,0:T(8,128)(2,1)} %param.15), channel_id=1, replica_groups=mesh['group_0'=8,'group_1'=4,'group_2'=2,'section'=4] {'section'}, dimensions={0}, use_global_device_ids=true | all-gather | bytes 573440 | tf_op jit(solution)/shard_map/all_gather | solution.py:181
  35.4 77.6 %all-gather.5.cloned.1.call-done = bf16[64,28,4096]{2,1,0:T(8,128)(2,1)} async-done(((bf16[1,28,4096]{2,1,0:T(8,128)(2,1)}), bf16[64,28,4096]{2,1,0:T(8,128)(2,1)}) %all-gather.5.cloned.1.call-update) | async-done | bytes 14680080 | tf_op jit(solution)/shard_map/all_gather | solution.py:28
  113.0 17.5 %reshape.792 = bf16[1792,4096]{1,0:T(8,128)(2,1)} reshape(bf16[64,28,4096]{2,1,0:T(8,128)(2,1)} %all-gather.5.cloned.1.call-done) | data formatting | bytes 29360128
  139.0 4.7 bitcast_dynamic-update-slice_fusion
  153.1 4.1 convolution_add_fusion.11
  158.9 4.7 fusion.133
  172.4 4.1 convolution_add_fusion.9
  178.2 4.7 fusion.131
  197.6 4.7 fusion.129
  211.1 4.1 convolution_add_fusion.5
  216.9 4.7 fusion.127
  230.5 4.1 convolution_add_fusion.3
  236.3 4.7 fusion.125
  249.8 4.1 convolution_add_fusion.1
  255.6 4.7 fusion.16
  260.3 4.9 %all-to-all-start = ((bf16[4,32,1792]{2,1,0:T(8,128)(2,1)}), bf16[4,32,1792]{2,1,0:T(8,128)(2,1)S(1)}, u32[]{:S(2)}, u32[]{:S(2)}) async-start(bf16[4,32,1792]{2,1,0:T(8,128)(2,1)} %fusion.16), calls=%async_computation | async-start | bytes 917504 | tf_op jit(solution)/shard_map/all_to_all | solution.py:234
  265.3 6.2 %all-to-all-done = bf16[4,32,1792]{2,1,0:T(8,128)(2,1)S(1)} async-done(((bf16[4,32,1792]{2,1,0:T(8,128)(2,1)}), bf16[4,32,1792]{2,1,0:T(8,128)(2,1)S(1)}, u32[]{:S(2)}, u32[]{:S(2)}) %all-to-all-start) | async-done | bytes 458784 | tf_op jit(solution)/shard_map/all_to_all | solution.py:234
  275.1 8.7 %all-to-all-start.1 = ((bf16[256,4,1792]{2,1,0:T(4,128)(2,1)}), bf16[256,4,1792]{2,1,0:T(4,128)(2,1)}, u32[]{:S(2)}, u32[]{:S(2)}) async-start(bf16[256,4,1792]{2,1,0:T(4,128)(2,1)} %stack.2), calls=%async_computation.1 | async-start | bytes 7340032 | tf_op jit(solution)/shard_map/all_to_all | solution.py:246
  284.1 142.5 %all-gather.2 = s32[256,4,3]{2,1,0:T(4,128)S(1)} all-gather(s32[1,4,3]{2,1,0:T(4,128)S(1)} %bitcast.454), channel_id=1, replica_groups=mesh['group_0'=8,'group_1'=4,'group_2'=2,'section'=4] {'group_0','group_..., dimensions={0}, use_global_device_ids=true | all-gather | bytes 12336 | tf_op jit(solution)/shard_map/all_gather | solution.py:37
  428.2 6.9 %reshape.777 = bf16[1024,1792]{1,0:T(8,128)(2,1)} reshape(bf16[256,4,1792]{2,1,0:T(4,128)(2,1)} %all-to-all-done.1) | data formatting | bytes 7340032 | tf_op jit(solution)/shard_map/reshape | solution.py:245
  438.5 15.3 %psum.28 = f32[1024]{0:T(1024)S(1)} all-reduce(f32[1024]{0:T(1024)S(1)} %fusion.31), channel_id=1, replica_groups=mesh['group_0'=8,'group_1'=4,'group_2'=2,'section'=4] {'group_0'}, use_global_device_ids=true, to_apply=%region_28.29 | all-reduce | flops 1024 | bytes 8192 | tf_op jit(solution)/shard_map/psum | solution.py:45
  453.8 8.0 %psum.29 = f32[1024]{0:T(1024)S(1)} all-reduce(f32[1024]{0:T(1024)S(1)} %psum.28), channel_id=1, replica_groups=mesh['group_0'=8,'group_1'=4,'group_2'=2,'section'=4] {'group_1'}, use_global_device_ids=true, to_apply=%region_29.30 | all-reduce | flops 1024 | bytes 8192 | tf_op jit(solution)/shard_map/psum | solution.py:45
  464.3 9.5 %psum.31 = f32[1024]{0:T(1024)S(1)} all-reduce(f32[1024]{0:T(1024)S(1)} %psum.30), channel_id=1, replica_groups=mesh['group_0'=8,'group_1'=4,'group_2'=2,'section'=4] {'section'}, use_global_device_ids=true, to_apply=%region_31.32 | all-reduce | flops 1024 | bytes 8192 | tf_op jit(solution)/shard_map/psum | solution.py:45
  (195 shorter events, 95.3 us)
Async XLA Ops:
  7.2 427.9 %copy-start = (bf16[304,1792]{1,0:T(8,128)(2,1)S(1)}, bf16[304,1792]{1,0:T(8,128)(2,1)}, u32[]{:S(2)}) copy-start(bf16[304,1792]{1,0:T(8,128)(2,1)} %param.29) | copy-start | bytes 3268612
  7.2 105.8 %all-gather.5.cloned.1.call-start = ((), (), s32[]{:S(2)}) async-start(), calls=%async_computation.2 | async-start | bytes 17039360 | tf_op jit(solution)/shard_map/all_gather | solution.py:28
  35.4 97.0 %copy-start.2 = (f32[1,256]{1,0:T(1,128)S(1)}, f32[1,256]{1,0:T(1,128)}, u32[]{:S(2)}) copy-start(f32[1,256]{1,0:T(1,128)} %param.26) | copy-start | bytes 3076
  35.4 97.0 %copy-start.3 = (f32[1,256]{1,0:T(1,128)S(1)}, f32[1,256]{1,0:T(1,128)}, u32[]{:S(2)}) copy-start(f32[1,256]{1,0:T(1,128)} %param.25) | copy-start | bytes 3076
  136.7 14.2 %copy-start.1 = (bf16[1,4,32,1792]{3,2,1,0:T(8,128)(2,1)S(1)}, bf16[1,4,32,1792]{3,2,1,0:T(8,128)(2,1)}, u32[]{:S(2)}) copy-start(bf16[1,4,32,1792]{3,2,1,0:T(8,128)(2,1)} %param.16) | copy-start | bytes 1376260
  143.7 7.2 %collective-permute-start = (bf16[32,1792]{1,0:T(8,128)(2,1)S(1)}, bf16[32,1792]{1,0:T(8,128)(2,1)S(1)}, u32[]{:S(2)}, u32[]{:S(2)}) collective-permute-start(bf16[32,1792]{1,0:T(8,128)(2,1)S(1)} %get-tuple-element.124), channel_id=1, source_target_pairs={{0,1},{1,2},{2,3},{4,5},{5,6},{6,7},{8,9},{9,10},{10,11},{12,13},{... | collective-permute-start | bytes 344072 | tf_op jit(solution)/shard_map/ppermute | solution.py:22
  163.6 6.7 %collective-permute-start.1 = (bf16[32,1792]{1,0:T(8,128)(2,1)S(1)}, bf16[32,1792]{1,0:T(8,128)(2,1)S(1)}, u32[]{:S(2)}, u32[]{:S(2)}) collective-permute-start(bf16[32,1792]{1,0:T(8,128)(2,1)S(1)} %get-tuple-element.126), channel_id=1, source_target_pairs={{0,1},{1,2},{2,3},{4,5},{5,6},{6,7},{8,9},{9,10},{10,11},{12,13},{... | collective-permute-start | bytes 344072 | tf_op jit(solution)/shard_map/ppermute | solution.py:22
  182.9 6.7 %collective-permute-start.2 = (bf16[32,1792]{1,0:T(8,128)(2,1)S(1)}, bf16[32,1792]{1,0:T(8,128)(2,1)S(1)}, u32[]{:S(2)}, u32[]{:S(2)}) collective-permute-start(bf16[32,1792]{1,0:T(8,128)(2,1)S(1)} %get-tuple-element.128), channel_id=1, source_target_pairs={{0,1},{1,2},{2,3},{4,5},{5,6},{6,7},{8,9},{9,10},{10,11},{12,13},{... | collective-permute-start | bytes 344072 | tf_op jit(solution)/shard_map/ppermute | solution.py:22
  202.3 6.7 %collective-permute-start.3 = (bf16[32,1792]{1,0:T(8,128)(2,1)S(1)}, bf16[32,1792]{1,0:T(8,128)(2,1)S(1)}, u32[]{:S(2)}, u32[]{:S(2)}) collective-permute-start(bf16[32,1792]{1,0:T(8,128)(2,1)S(1)} %get-tuple-element.130), channel_id=1, source_target_pairs={{0,1},{1,2},{2,3},{4,5},{5,6},{6,7},{8,9},{9,10},{10,11},{12,13},{... | collective-permute-start | bytes 344072 | tf_op jit(solution)/shard_map/ppermute | solution.py:22
  221.6 6.7 %collective-permute-start.4 = (bf16[32,1792]{1,0:T(8,128)(2,1)S(1)}, bf16[32,1792]{1,0:T(8,128)(2,1)S(1)}, u32[]{:S(2)}, u32[]{:S(2)}) collective-permute-start(bf16[32,1792]{1,0:T(8,128)(2,1)S(1)} %get-tuple-element.132), channel_id=1, source_target_pairs={{0,1},{1,2},{2,3},{4,5},{5,6},{6,7},{8,9},{9,10},{10,11},{12,13},{... | collective-permute-start | bytes 344072 | tf_op jit(solution)/shard_map/ppermute | solution.py:22
  234.6 10.0 %copy-start.7 = (s32[1,5]{1,0:T(1,128)S(1)}, s32[1,5]{1,0:T(1,128)}, u32[]{:S(2)}) copy-start(s32[1,5]{1,0:T(1,128)} %param.17) | copy-start | bytes 64
  241.0 6.7 %collective-permute-start.5 = (bf16[32,1792]{1,0:T(8,128)(2,1)S(1)}, bf16[32,1792]{1,0:T(8,128)(2,1)S(1)}, u32[]{:S(2)}, u32[]{:S(2)}) collective-permute-start(bf16[32,1792]{1,0:T(8,128)(2,1)S(1)} %get-tuple-element.134), channel_id=1, source_target_pairs={{0,1},{1,2},{2,3},{4,5},{5,6},{6,7},{8,9},{9,10},{10,11},{12,13},{... | collective-permute-start | bytes 344072 | tf_op jit(solution)/shard_map/ppermute | solution.py:22
  254.1 18.2 %copy-start.4 = (f32[1792]{0:T(1024)S(1)}, f32[1792]{0:T(1024)}, u32[]{:S(2)}) copy-start(f32[1792]{0:T(1024)} %param.28) | copy-start | bytes 21508
  260.3 23.5 %copy-start.5 = (s32[1,4]{1,0:T(1,128)S(1)}, s32[1,4]{1,0:T(1,128)}, u32[]{:S(2)}) copy-start(s32[1,4]{1,0:T(1,128)} %param.19) | copy-start | bytes 52
  260.3 23.5 %copy-start.6 = (s32[1,4]{1,0:T(1,128)S(1)}, s32[1,4]{1,0:T(1,128)}, u32[]{:S(2)}) copy-start(s32[1,4]{1,0:T(1,128)} %param.18) | copy-start | bytes 52
  260.3 23.7 %copy-start.8 = (s32[1,4,2]{1,2,0:T(2,128)S(1)}, s32[1,4,2]{1,2,0:T(2,128)}, u32[]{:S(2)}) copy-start(s32[1,4,2]{1,2,0:T(2,128)} %param.20) | copy-start | bytes 100
  260.3 11.2 %all-to-all-start = ((bf16[4,32,1792]{2,1,0:T(8,128)(2,1)}), bf16[4,32,1792]{2,1,0:T(8,128)(2,1)S(1)}, u32[]{:S(2)}, u32[]{:S(2)}) async-start(bf16[4,32,1792]{2,1,0:T(8,128)(2,1)} %fusion.16), calls=%async_computation | async-start | bytes 917504 | tf_op jit(solution)/shard_map/all_to_all | solution.py:234
  275.1 153.1 %all-to-all-start.1 = ((bf16[256,4,1792]{2,1,0:T(4,128)(2,1)}), bf16[256,4,1792]{2,1,0:T(4,128)(2,1)}, u32[]{:S(2)}, u32[]{:S(2)}) async-start(bf16[256,4,1792]{2,1,0:T(4,128)(2,1)} %stack.2), calls=%async_computation.1 | async-start | bytes 7340032 | tf_op jit(solution)/shard_map/all_to_all | solution.py:246
Sparse Core Ops, SparseCore 0:
  10.8 102.1 all-gather.4
